TPU v7x, 32 devices: a whole 2x2x4 slice. The times are simulated.
32 devices in a mesh: gx: 4 (over y, core), gy: 8 (over z, x).
Axes of the slice: x: 2, y: 2, z: 4, core: 2. Of those that a mesh axis runs over, the one named last changes fastest.
Arguments:
- transfer: bfloat16 [512, 75, 128], P(('gx', 'gy')), may hold values from -6 to 6
- positions: float32 [512, 3, 128], P(('gx', 'gy')), may hold values from -4 to 4
- normals: float32 [512, 3, 128], P(('gx', 'gy')), may hold values from -4 to 4
- area: float32 [512, 128], P(('gx', 'gy')), may hold values from 0.06 to 3
- albedo: float32 [512, 3, 128], P(('gx', 'gy')), may hold values from 0.3 to 0.9
- pairs: int32 [512, 40], P(('gx', 'gy')), may hold values from 0 to 511, as said below
- home: int32 [512], replicated, may hold values from 0 to 511, as said below
Outputs:
- bounce_one: bfloat16 [512, 75, 128], P(('gx', 'gy'))
- bounce_two: bfloat16 [512, 75, 128], P(('gx', 'gy'))
- energies: float32 [2], replicated
Inputs may be any that keep to these rules, and one draw needn't show every extreme that they name: `home`: A permutation; the block in slot s is held by device s // 16, devices counted gx major. `pairs`: the first 16 entries of a row name blocks held by the same device as the row's slot, the other 24 name blocks held by other devices. Over the rows of one device, the far entries name at most 2 distinct blocks of any one other device, and exactly 2 of some. Ids may repeat within a row; each entry counts.
All inputs are finite; a program needn't handle non-finite values.
Results may differ from a plain program's by a relative error of at most 0.02.
Values may be sent and summed in bfloat16 or wider, within the bound.
A program may use at most 128 MiB of HBM per device.

v0:
```python
import functools

import jax
import jax.numpy as jnp
from jax import lax
from jax.experimental import pallas as pl
from jax.experimental.pallas import tpu as pltpu
from jax.sharding import PartitionSpec as P

COLORS = 3
NEAR = 16
CAP = 2
AXES = ("gx", "gy")
GEO = 16
VMEM_LIMIT = 62 * 1024 * 1024
MESH = pl.DeviceIdType.MESH


def split3(f):
    hi = f.astype(jnp.bfloat16).astype(jnp.float32)
    rest = f - hi
    mid = rest.astype(jnp.bfloat16).astype(jnp.float32)
    return hi, mid, rest - mid


def source_features(pos, nrm, area):
    lanes = pos.shape[1]
    m = nrm * (area * (1.0 / jnp.pi))
    sq = jnp.sum(pos * pos, axis=0, keepdims=True)
    d = -jnp.sum(m * pos, axis=0, keepdims=True)
    feat = jnp.concatenate([pos, sq, m, d], axis=0)
    hi, mid, lo = split3(feat)
    ones = jnp.ones((8, lanes), jnp.float32)
    half = jnp.concatenate([hi, hi, hi, mid, mid, lo, ones, jnp.zeros_like(ones)], axis=0)
    return jnp.concatenate([half, half], axis=0).T


def receiver_weights(pos, nrm):
    lanes = pos.shape[1]
    zero3 = jnp.zeros((3, lanes), jnp.float32)
    zero1 = jnp.zeros((1, lanes), jnp.float32)
    one1 = jnp.ones((1, lanes), jnp.float32)
    zero5 = jnp.zeros((5, lanes), jnp.float32)
    zero8 = jnp.zeros((8, lanes), jnp.float32)

    def column(feat, const):
        hi, mid, lo = split3(feat)
        chi, cmid, clo = split3(const)
        return jnp.concatenate(
            [hi, mid, lo, hi, mid, hi, jnp.concatenate([chi, cmid, clo, zero5], axis=0), zero8],
            axis=0,
        )

    dist = column(
        jnp.concatenate([-2.0 * pos, one1, zero3, zero1], axis=0),
        jnp.sum(pos * pos, axis=0, keepdims=True) + 1.0,
    )
    along_p = column(
        jnp.concatenate([nrm, zero1, zero3, zero1], axis=0),
        -jnp.sum(nrm * pos, axis=0, keepdims=True),
    )
    along_q = column(jnp.concatenate([zero3, zero1, pos, one1], axis=0), zero1)
    return jnp.concatenate([dist, along_p, along_q], axis=1)


def block_diag(w):
    z = jnp.zeros_like(w)
    return jnp.concatenate(
        [jnp.concatenate([w, z], axis=1), jnp.concatenate([z, w], axis=1)], axis=0
    ).astype(jnp.bfloat16)


def albedo_rows(alb, rows, per_color):
    r = lax.broadcasted_iota(jnp.int32, (rows, alb.shape[1]), 0)
    out = jnp.broadcast_to(alb[COLORS - 1 : COLORS, :], (rows, alb.shape[1]))
    for c in range(COLORS - 2, -1, -1):
        out = jnp.where(r < (c + 1) * per_color, alb[c : c + 1, :], out)
    return out


def fill_table(geom, count, feats):
    def one(t, carry):
        feats[t] = source_features(*geom(t)).astype(jnp.bfloat16)
        return carry

    lax.fori_loop(0, count, one, 0)


def row_tiles(rows_ref, slot, base, weights, feats, tiles):
    v = tiles.shape[-1]
    first = lax.broadcasted_iota(jnp.int32, (v, v), 1) < v // 2
    for i in range(rows_ref.shape[1] // 4):
        t = [rows_ref[slot, i * 4 + j] for j in range(4)]
        x = jnp.concatenate(
            [
                jnp.where(first, feats[t[0]], feats[t[1]]),
                jnp.where(first, feats[t[2]], feats[t[3]]),
            ],
            axis=0,
        )
        g = jnp.dot(x, weights, preferred_element_type=jnp.float32)
        for j in range(4):
            r, c = (j // 2) * v, (j % 2) * 3 * v
            dist = g[r : r + v, c : c + v]
            ap = g[r : r + v, c + v : c + 2 * v]
            aq = g[r : r + v, c + 2 * v : c + 3 * v]
            f = jnp.maximum(ap, 0.0) * jnp.maximum(aq, 0.0) / (dist * dist)
            at = base + (i * 4 + j) * v
            tiles[slot, at : at + v, :] = f.astype(jnp.bfloat16)


def contract(rows_ref, slot, base, load, tiles):
    v = tiles.shape[-1]
    count = rows_ref.shape[1]
    picked = jnp.concatenate([load(rows_ref[slot, j]) for j in range(count)], axis=1)
    return jnp.dot(
        picked, tiles[slot, base : base + count * v, :], preferred_element_type=jnp.float32
    )


def bounce_kernel(
    n, ny,
    near_rows, far_rows, asked,
    transfer, pos, nrm, area, alb,
    one_ref, two_ref, energy_ref,
    local, geo_local, geo_out, geo_in, box_out, box_in, box_in2,
    near_feats, far_feats, tiles, acc, one, en, en_in,
    gs, gr, rs, rr, ss, sr, e1s, e1r, e2s, e2r,
):
    bf16, f32 = jnp.bfloat16, jnp.float32
    me = lax.axis_index("gx") * ny + lax.axis_index("gy")
    b, ch, v = transfer.shape
    rows = local.shape[1]
    near = near_rows.shape[1]

    def peer(d):
        t = lax.rem(me + d, n)
        return t, (t // ny, lax.rem(t, ny))

    def each_peer(fn):
        def step(d, carry):
            fn(d)
            return carry

        lax.fori_loop(1, n, step, 0)

    def copies(src, dst, send, recv):
        def make(d):
            t, dev = peer(d)
            return pltpu.make_async_remote_copy(
                src_ref=src(t), dst_ref=dst, send_sem=send.at[d], recv_sem=recv.at[d],
                device_id=dev, device_id_type=MESH,
            )

        return make

    def pair(ref, t):
        return ref.at[pl.ds(t * CAP, CAP)]

    geo_cp = copies(lambda t: pair(geo_out, t), pair(geo_in, me), gs, gr)
    rad_cp = copies(lambda t: pair(box_out, t), pair(box_in, me), rs, rr)
    sec_cp = copies(lambda t: pair(box_out, t), pair(box_in2, me), ss, sr)
    e1_cp = copies(lambda t: en.at[0], en_in.at[0, me], e1s, e1r)
    e2_cp = copies(lambda t: en.at[1], en_in.at[1, me], e2s, e2r)

    barrier = pltpu.get_barrier_semaphore()
    each_peer(lambda d: pl.semaphore_signal(barrier, inc=1, device_id=peer(d)[1], device_id_type=MESH))

    def stage(t, carry):
        local[t] = jnp.concatenate(
            [transfer[t], jnp.zeros((rows - ch, v), bf16)], axis=0
        )
        p_hi, p_mid, _ = split3(pos[t])
        n_hi, n_mid, _ = split3(nrm[t])
        geo_local[t] = jnp.concatenate(
            [p_hi, p_mid, n_hi, n_mid, area[t], jnp.zeros((GEO - 13, v), f32)], axis=0
        ).astype(bf16)
        return carry

    lax.fori_loop(0, b, stage, 0)

    def pack(source, out):
        def step(t, carry):
            for k in range(CAP):
                out[t * CAP + k] = source[asked[t * CAP + k]]
            return carry

        lax.fori_loop(0, n, step, 0)

    pack(geo_local, geo_out)
    pack(local, box_out)
    for box in (geo_in, box_in, box_in2):
        for k in range(CAP):
            box[me * CAP + k] = jnp.zeros(box.shape[1:], bf16)
    pl.semaphore_wait(barrier, n - 1)
    each_peer(lambda d: geo_cp(d).start())
    each_peer(lambda d: rad_cp(d).start())

    def weights_of(s):
        return block_diag(receiver_weights(pos[s], nrm[s]))

    fill_table(lambda t: (pos[t], nrm[t], area[t]), b, near_feats)

    def near_slot(s, carry):
        row_tiles(near_rows, s, 0, weights_of(s), near_feats, tiles)
        return carry

    def near_sum(table):
        def step(s, carry):
            acc[s] = contract(near_rows, s, 0, lambda t: table[t], tiles)
            return carry

        lax.fori_loop(0, b, step, 0, unroll=2)

    lax.fori_loop(0, b, near_slot, 0)
    near_sum(local)
    each_peer(lambda d: geo_cp(d).wait())

    def far_geom(t):
        g = geo_in[t].astype(f32)
        return g[0:3] + g[3:6], g[6:9] + g[9:12], g[12:13]

    fill_table(far_geom, n * CAP, far_feats)

    def far_slot(s, carry):
        row_tiles(far_rows, s, near * v, weights_of(s), far_feats, tiles)
        return carry

    lax.fori_loop(0, b, far_slot, 0)
    each_peer(lambda d: rad_cp(d).wait())

    def finish(s, box, e):
        total = acc[s] + contract(far_rows, s, near * v, lambda t: box[t], tiles)
        val = total * albedo_rows(alb[s], rows, ch // COLORS)
        r = lax.broadcasted_iota(jnp.int32, val.shape, 0)
        part = jnp.sum(jnp.where(r < ch, val * val * area[s], 0.0), axis=0, keepdims=True)
        return val.astype(bf16), e + part

    def first_slot(s, e):
        val, e = finish(s, box_in, e)
        one[s] = val
        one_ref[s] = val[0:ch]
        return e

    zero = jnp.zeros((1, v), f32)
    row0 = lax.broadcasted_iota(jnp.int32, (8, v), 0) == 0
    e1 = lax.fori_loop(0, b, first_slot, zero, unroll=2)
    pack(one, box_out)
    each_peer(lambda d: sec_cp(d).start())
    en[0] = jnp.where(row0, e1, 0.0)
    en_in[0, me] = en[0]

    near_sum(one)
    each_peer(lambda d: e1_cp(d).start())
    each_peer(lambda d: sec_cp(d).wait())

    def second_slot(s, e):
        val, e = finish(s, box_in2, e)
        two_ref[s] = val[0:ch]
        return e

    e2 = lax.fori_loop(0, b, second_slot, zero, unroll=2)
    en[1] = jnp.where(row0, e2, 0.0)
    en_in[1, me] = en[1]
    each_peer(lambda d: e2_cp(d).start())
    each_peer(lambda d: e1_cp(d).wait())
    each_peer(lambda d: e2_cp(d).wait())
    energy_ref[...] = jnp.sum(en_in[...], axis=1)


def body(transfer, positions, normals, area, albedo, pairs, home):
    n = lax.axis_size(AXES)
    me = lax.axis_index(AXES)
    b, ch, v = transfer.shape
    far = pairs.shape[1] - NEAR
    rows = -(-ch // 16) * 16
    bf16, f32 = jnp.bfloat16, jnp.float32

    ids = jnp.arange(home.shape[0], dtype=jnp.int32)
    slot_ids = jnp.sum(jnp.where(pairs[:, :, None] == ids, home, 0), axis=2)
    near_rows = slot_ids[:, :NEAR] - me * b
    far_ids = slot_ids[:, NEAR:]
    owner = far_ids // b
    here = far_ids - owner * b
    devs = jnp.arange(n, dtype=jnp.int32)
    mine = owner[:, :, None] == devs
    low = jnp.min(jnp.where(mine, here[:, :, None], b - 1), axis=(0, 1))
    high = jnp.max(jnp.where(mine, here[:, :, None], 0), axis=(0, 1))
    low_of = jnp.sum(jnp.where(mine, low, 0), axis=2)
    far_rows = owner * CAP + (here > low_of).astype(jnp.int32)
    asked = lax.all_to_all(
        jnp.stack([low, high], axis=1), AXES, split_axis=0, concat_axis=0, tiled=True
    ).reshape(-1)

    vmem = pl.BlockSpec(memory_space=pltpu.VMEM)
    smem = pl.BlockSpec(memory_space=pltpu.SMEM)
    sem = pltpu.SemaphoreType.DMA((n,))
    one, two, energy = pl.pallas_call(
        functools.partial(bounce_kernel, n, lax.axis_size("gy")),
        name="bounces",
        in_specs=[smem] * 3 + [vmem] * 5,
        out_specs=[vmem] * 3,
        out_shape=[
            jax.ShapeDtypeStruct((b, ch, v), bf16),
            jax.ShapeDtypeStruct((b, ch, v), bf16),
            jax.ShapeDtypeStruct((2, 8, v), f32),
        ],
        scratch_shapes=[
            pltpu.VMEM((b, rows, v), bf16),
            pltpu.VMEM((b, GEO, v), bf16),
            pltpu.VMEM((n * CAP, GEO, v), bf16),
            pltpu.VMEM((n * CAP, GEO, v), bf16),
            pltpu.VMEM((n * CAP, rows, v), bf16),
            pltpu.VMEM((n * CAP, rows, v), bf16),
            pltpu.VMEM((n * CAP, rows, v), bf16),
            pltpu.VMEM((b, v, v), bf16),
            pltpu.VMEM((n * CAP, v, v), bf16),
            pltpu.VMEM((b, (NEAR + far) * v, v), bf16),
            pltpu.VMEM((b, rows, v), f32),
            pltpu.VMEM((b, rows, v), bf16),
            pltpu.VMEM((2, 8, v), f32),
            pltpu.VMEM((2, n, 8, v), f32),
        ]
        + [sem] * 10,
        compiler_params=pltpu.CompilerParams(
            collective_id=0, has_side_effects=True, vmem_limit_bytes=VMEM_LIMIT
        ),
    )(near_rows, far_rows, asked, transfer, positions, normals, area[:, None, :], albedo)
    energies = jnp.sum(energy, axis=(1, 2)) * (1.0 / (n * b * v * ch))
    return one, two, energies


def solution(mesh):
    return jax.shard_map(
        body,
        mesh=mesh,
        in_specs=(
            P(AXES, None, None),
            P(AXES, None, None),
            P(AXES, None, None),
            P(AXES, None),
            P(AXES, None, None),
            P(AXES, None),
            P(),
        ),
        out_specs=(P(AXES, None, None), P(AXES, None, None), P()),
        check_vma=False,
    )
```

profile of v0, /device:TPU:0, one launch (start us, length us, event | category | flops | bytes accessed | tf_op | source)
XLA Modules:
  0.0 112.2 jit_solution(10254522770237146731)
XLA Ops:
  0.6 0.0 copy-start.2
  0.7 1.2 %select_reduce_fusion = s32[16,40]{1,0:T(8,128)S(1)} fusion(s32[512]{0:T(512)} %param.13, s32[16,40]{1,0:T(8,128)} %param.12), kind=kLoop, calls=%fused_computation | loop fusion | flops 982400 | bytes 7168 | tf_op jit(solution)/shard_map/reduce_sum | solution.py:280
  1.9 0.1 add_select_fusion
  2.0 0.2 select_reduce_fusion.1
  2.2 0.7 copy.31
  2.9 7.3 %all-to-all-start = ((s32[32,1,2]{2,1,0:T(1,128)}), s32[32,1,2]{2,1,0:T(1,128)S(1)}, u32[]{:S(2)}, u32[]{:S(2)}) async-start(s32[32,1,2]{2,1,0:T(1,128)} %copy.31), calls=%async_computation | async-start | bytes 32768 | tf_op jit(solution)/shard_map/all_to_all | solution.py:291
  10.2 0.4 select_reduce_fusion.2
  10.7 0.7 convert_add_fusion.far_rows
  11.3 0.6 slice_subtract_fusion.near_rows
  11.9 1.4 %copy.33.pos = f32[16,3,128]{2,1,0:T(4,128)} copy(f32[16,3,128]{2,0,1:T(8,128)} %param.8) | data formatting | bytes 49152 | tf_op args[1]
  13.3 1.4 %copy.34.nrm = f32[16,3,128]{2,1,0:T(4,128)} copy(f32[16,3,128]{2,0,1:T(8,128)} %param.9) | data formatting | bytes 49152 | tf_op args[2]
  14.7 0.0 copy-done.2
  14.7 0.6 copy.35.alb
  15.3 0.8 copy.32.transfer
  16.1 1.2 %all-to-all-done = s32[32,1,2]{2,1,0:T(1,128)S(1)} async-done(((s32[32,1,2]{2,1,0:T(1,128)}), s32[32,1,2]{2,1,0:T(1,128)S(1)}, u32[]{:S(2)}, u32[]{:S(2)}) %all-to-all-start) | async-done | bytes 288 | tf_op jit(solution)/shard_map/all_to_all | solution.py:291
  17.3 0.5 broadcast.24
  17.9 0.7 reduce.3
  18.5 0.6 reshape.15.asked
  19.2 89.8 %bounces.1 = (bf16[16,75,128]{2,1,0:T(8,128)(2,1)}, bf16[16,75,128]{2,1,0:T(8,128)(2,1)}, f32[2,8,128]{2,1,0:T(8,128)}) custom-call(s32[16,16]{1,0:T(8,128)} %slice_subtract_fusion.near_rows, s32[16,24]{1,0:T(8,128)} %convert_add_fusion.far_rows, s32[64]{0:T(128)} %reshape.15.asked, bf16[16,75,128]{2,1,0:T(8,128)(2,1)} %copy.32.transfer, ...), custom_call_target="tpu_custom_call" | custom-call | tf_op jit(solution)/shard_map/bounces/pallas_call | solution.py:298
  109.0 1.8 %copy.36 = bf16[16,75,128]{2,0,1:T(8,128)(2,1)} copy(bf16[16,75,128]{2,1,0:T(8,128)(2,1)} %get-tuple-element.18) | data formatting | bytes 614400
  110.8 0.0 copy-done.3
  110.8 0.1 reduce_sum.29
  110.9 0.5 broadcast_multiply_fusion
  111.4 0.8 copy.37
  (6 shorter events, 0.0 us)
Async XLA Ops:
  0.6 14.0 %copy-start.2 = (f32[16,3,128]{2,0,1:T(8,128)S(1)}, f32[16,3,128]{2,0,1:T(8,128)}, u32[]{:S(2)}) copy-start(f32[16,3,128]{2,0,1:T(8,128)} %param.11) | copy-start | bytes 73732
  0.6 14.7 %copy-start.1 = (bf16[16,75,128]{2,0,1:T(8,128)(2,1)S(1)}, bf16[16,75,128]{2,0,1:T(8,128)(2,1)}, u32[]{:S(2)}) copy-start(bf16[16,75,128]{2,0,1:T(8,128)(2,1)} %param.7) | copy-start | bytes 921604
  2.9 14.5 %all-to-all-start = ((s32[32,1,2]{2,1,0:T(1,128)}), s32[32,1,2]{2,1,0:T(1,128)S(1)}, u32[]{:S(2)}, u32[]{:S(2)}) async-start(s32[32,1,2]{2,1,0:T(1,128)} %copy.31), calls=%async_computation | async-start | bytes 32768 | tf_op jit(solution)/shard_map/all_to_all | solution.py:291
  109.0 1.8 %copy-start.3 = (f32[2,8,128]{2,1,0:T(8,128)S(1)}, f32[2,8,128]{2,1,0:T(8,128)}, u32[]{:S(2)}) copy-start(f32[2,8,128]{2,1,0:T(8,128)} %get-tuple-element.8) | copy-start | bytes 24580
  109.0 2.4 %copy-start = (bf16[16,75,128]{2,1,0:T(8,128)(2,1)S(1)}, bf16[16,75,128]{2,1,0:T(8,128)(2,1)}, u32[]{:S(2)}) copy-start(bf16[16,75,128]{2,1,0:T(8,128)(2,1)} %get-tuple-element.19) | copy-start | bytes 921604
where the time goes:
time: 112 us
  Pallas kernels  89.8 us (80%)
  local copies, waits for them, and re-layouts  8.6 us (8%)
  starting transfers between devices  7.33 us (7%)
  other arithmetic  4.54 us (4%)
  waiting for transfers between devices  1.24 us (1%)
    pallas_call x1, Pallas kernels, body(): pl.pallas_call(functools.partial(bounce_kernel, n, lax.axis_size('gy')),...  89.8 us
    all_to_all x1, starting transfers between devices, body(): lax.all_to_all(jnp.stack([low, high], axis=1), AXES, split_axis=0, concat...  7.33 us
    unnamed x14, local copies, waits for them, and re-layouts  6.78 us
  transfers between devices with their start and end apart: 1, of which 1 were waited for; matrix products, arithmetic and copies ran while one was open for 5% of the time, Pallas kernels for 0%

commit v1 on v0

v1 whole, which is shorter than its diff:
```python
import functools

import jax
import jax.numpy as jnp
from jax import lax
from jax.experimental import pallas as pl
from jax.experimental.pallas import tpu as pltpu
from jax.sharding import PartitionSpec as P

COLORS = 3
NEAR = 16
CAP = 2
AXES = ("gx", "gy")
VMEM_LIMIT = 62 * 1024 * 1024
MESH = pl.DeviceIdType.MESH


def split3(f):
    hi = f.astype(jnp.bfloat16).astype(jnp.float32)
    rest = f - hi
    mid = rest.astype(jnp.bfloat16).astype(jnp.float32)
    return hi, mid, rest - mid


def source_features(pos, m):
    lanes = pos.shape[1]
    sq = jnp.sum(pos * pos, axis=0, keepdims=True)
    d = -jnp.sum(m * pos, axis=0, keepdims=True)
    hi, mid, lo = split3(jnp.concatenate([pos, sq, m, d], axis=0))
    ones = jnp.ones((8, lanes), jnp.float32)
    half = jnp.concatenate([hi, hi, hi, mid, mid, lo, ones, jnp.zeros_like(ones)], axis=0)
    return jnp.concatenate([half, half], axis=0).T


def receiver_weights(pos, nrm):
    lanes = pos.shape[1]
    zero3 = jnp.zeros((3, lanes), jnp.float32)
    zero1 = jnp.zeros((1, lanes), jnp.float32)
    one1 = jnp.ones((1, lanes), jnp.float32)
    zero5 = jnp.zeros((5, lanes), jnp.float32)
    zero8 = jnp.zeros((8, lanes), jnp.float32)

    def column(feat, const):
        hi, mid, lo = split3(feat)
        chi, cmid, clo = split3(const)
        return jnp.concatenate(
            [hi, mid, lo, hi, mid, hi, jnp.concatenate([chi, cmid, clo, zero5], axis=0), zero8],
            axis=0,
        )

    dist = column(
        jnp.concatenate([-2.0 * pos, one1, zero3, zero1], axis=0),
        jnp.sum(pos * pos, axis=0, keepdims=True) + 1.0,
    )
    along_p = column(
        jnp.concatenate([nrm, zero1, zero3, zero1], axis=0),
        -jnp.sum(nrm * pos, axis=0, keepdims=True),
    )
    along_q = column(jnp.concatenate([zero3, zero1, pos, one1], axis=0), zero1)
    return jnp.concatenate([dist, along_p, along_q], axis=1)


def block_diag(w):
    z = jnp.zeros_like(w)
    return jnp.concatenate(
        [jnp.concatenate([w, z], axis=1), jnp.concatenate([z, w], axis=1)], axis=0
    ).astype(jnp.bfloat16)


def row_tiles(rows_ref, slot, base, weights, feats, tiles):
    v = tiles.shape[-1]
    first = lax.broadcasted_iota(jnp.int32, (v, v), 1) < v // 2
    for i in range(rows_ref.shape[1] // 4):
        t = [rows_ref[slot, i * 4 + j] for j in range(4)]
        x = jnp.concatenate(
            [
                jnp.where(first, feats[t[0]], feats[t[1]]),
                jnp.where(first, feats[t[2]], feats[t[3]]),
            ],
            axis=0,
        )
        g = jnp.dot(x, weights, preferred_element_type=jnp.float32)
        for j in range(4):
            r, c = (j // 2) * v, (j % 2) * 3 * v
            dist = g[r : r + v, c : c + v]
            ap = g[r : r + v, c + v : c + 2 * v]
            aq = g[r : r + v, c + 2 * v : c + 3 * v]
            f = jnp.maximum(ap, 0.0) * jnp.maximum(aq, 0.0) / (dist * dist)
            at = base + (i * 4 + j) * v
            tiles[slot, at : at + v, :] = f.astype(jnp.bfloat16)


def contract(rows_ref, slot, base, field, tiles):
    v = tiles.shape[-1]
    count = rows_ref.shape[1]
    picked = jnp.concatenate([field[rows_ref[slot, j]] for j in range(count)], axis=1)
    return jnp.dot(
        picked, tiles[slot, base : base + count * v, :], preferred_element_type=jnp.float32
    )


def bounce_kernel(
    n, ny, ch, cuts,
    pairs, home, transfer, positions, normals, area, albedo,
    one_hbm, two_hbm, energy_ref,
    *scratch,
):
    (
        near_rows, far_ids, far_rows, low_s, req_s,
        tr, raw_pos, raw_nrm, raw_area, raw_alb, geo, wire, field,
        geo_out, geo_in, near_feats, far_feats, wts, tiles,
        req_v, req_in, acc, one, two, out1, out2, en, en_in,
    ) = scratch[:28]
    k = len(cuts)
    box_out = scratch[28 : 28 + k]
    box_in = scratch[28 + k : 28 + 2 * k]
    box_in2 = scratch[28 + 2 * k : 28 + 3 * k]
    sems = scratch[28 + 3 * k :]
    loc, pair_sems = sems[0], sems[1:]
    bf16, f32, i32 = jnp.bfloat16, jnp.float32, jnp.int32

    gx, gy = lax.axis_index("gx"), lax.axis_index("gy")
    me = gx * ny + gy
    b, v = area.shape
    near = near_rows.shape[1]
    far = far_ids.shape[1]

    def peer(d):
        t = lax.rem(me + d, n)
        return t, (lax.div(t, ny), lax.rem(t, ny))

    def each_peer(fn):
        def step(d, carry):
            fn(d)
            return carry

        lax.fori_loop(1, n, step, 0)

    def copies(which, src, dst):
        send, recv = pair_sems[2 * which], pair_sems[2 * which + 1]

        def make(d):
            t, dev = peer(d)
            return pltpu.make_async_remote_copy(
                src_ref=src(t), dst_ref=dst, send_sem=send.at[d], recv_sem=recv.at[d],
                device_id=dev, device_id_type=MESH,
            )

        return make

    def pair(ref, t):
        return ref.at[pl.ds(t * CAP, CAP)]

    req_cp = copies(0, lambda t: req_v.at[0], req_in.at[me])
    geo_cp = copies(1, lambda t: geo_out.at[t], geo_in.at[me])
    en_cp = copies(2, lambda t: en, en_in.at[me])

    def field_cp(i, which, box):
        return copies(which, lambda t: pair(box_out[i], t), pair(box[i], me))

    first_cp = [field_cp(i, 3 + i, box_in) for i in range(k)]
    second_cp = [field_cp(i, 3 + k + i, box_in2) for i in range(k)]

    barrier = pltpu.get_barrier_semaphore()
    each_peer(lambda d: pl.semaphore_signal(barrier, inc=1, device_id=peer(d)[1], device_id_type=MESH))
    loads = [
        pltpu.make_async_copy(src, dst, loc.at[i])
        for i, (src, dst) in enumerate(
            [
                (positions, raw_pos), (normals, raw_nrm), (area, raw_area),
                (albedo, raw_alb), (transfer, tr),
            ]
        )
    ]
    for cp in loads:
        cp.start()

    lanes = req_v.shape[2]
    floor = lax.broadcasted_iota(i32, (1, lanes), 1) * b

    def scan(s, carry):
        low, high = carry
        for j in range(near):
            near_rows[s, j] = lax.rem(home[pairs[s, j]], b)
        for j in range(far):
            t = home[pairs[s, near + j]]
            far_ids[s, j] = t
            x = t - floor
            ok = (x >= 0) & (x < b)
            low = jnp.minimum(low, jnp.where(ok, x, b - 1))
            high = jnp.maximum(high, jnp.where(ok, x, 0))
        return low, high

    low, high = lax.fori_loop(
        0, b, scan, (jnp.full((1, lanes), b - 1, i32), jnp.zeros((1, lanes), i32))
    )
    req_v[0] = low + high * b
    req_v[1] = low
    req_in[me] = jnp.zeros((1, lanes), i32)
    low_cp = pltpu.make_async_copy(req_v.at[1], low_s, loc.at[5])
    low_cp.start()

    for cp in loads[:4]:
        cp.wait()
    m = raw_nrm[...] * (raw_area[...] * (1.0 / jnp.pi))[None]
    p_hi, p_mid, _ = split3(raw_pos[...])
    m_hi, m_mid, _ = split3(m)
    geo[...] = jnp.swapaxes(
        jnp.concatenate(
            [raw_pos[...], m, raw_nrm[...], raw_area[...][None], raw_alb[...],
             jnp.zeros((3, b, v), f32)], axis=0
        ),
        0, 1,
    )
    wire[...] = jnp.swapaxes(
        jnp.concatenate([p_hi, p_mid, m_hi, m_mid, jnp.zeros((4, b, v), f32)], axis=0), 0, 1
    ).astype(bf16)
    loads[4].wait()
    for lo, hi in cuts:
        part = tr[lo : min(hi, ch)]
        if hi > ch:
            part = jnp.concatenate([part, jnp.zeros((hi - ch, b, v), bf16)], axis=0)
        field[:, lo:hi] = jnp.swapaxes(part, 0, 1)

    def table(read, count, feats):
        def step(t, carry):
            for i in range(4):
                feats[t * 4 + i] = source_features(*read(t * 4 + i)).astype(bf16)
            return carry

        lax.fori_loop(0, count // 4, step, 0)

    table(lambda t: (geo[t, 0:3], geo[t, 3:6]), b, near_feats)

    def near_slots(lo, hi):
        def step(s, carry):
            w = block_diag(receiver_weights(geo[s, 0:3], geo[s, 6:9]))
            wts[s] = w
            row_tiles(near_rows, s, 0, w, near_feats, tiles)
            return carry

        lax.fori_loop(lo, hi, step, 0, unroll=2)

    pl.semaphore_wait(barrier, n - 1)
    each_peer(lambda d: req_cp(d).start())
    near_slots(0, b // 4)
    for box in (geo_in,) + tuple(box_in) + tuple(box_in2):
        each = box.shape[0] // n
        for c in range(each):
            box[me * each + c] = jnp.zeros(box.shape[1:], box.dtype)
    each_peer(lambda d: req_cp(d).wait())
    ask_cp = pltpu.make_async_copy(req_in, req_s, loc.at[0])
    ask_cp.start()
    ask_cp.wait()

    def pack(put):
        def step(t, carry):
            r = req_s[t, 0, me]
            hi = lax.div(r, b)
            put(t, r - hi * b, hi)
            return carry

        lax.fori_loop(0, n, step, 0)

    def put_geo(t, x, y):
        geo_out[t] = jnp.concatenate([wire[x, 0:12], wire[y, 0:12]], axis=0)

    def put_field(i, source):
        lo, hi = cuts[i]

        def put(t, x, y):
            box_out[i][t * CAP] = source[x, lo:hi]
            box_out[i][t * CAP + 1] = source[y, lo:hi]

        return put

    pack(put_geo)
    each_peer(lambda d: geo_cp(d).start())
    for i in range(k):
        pack(put_field(i, field))
        each_peer(lambda d: first_cp[i](d).start())

    low_cp.wait()

    def far_index(s, carry):
        for j in range(far):
            t = far_ids[s, j]
            owner = lax.div(t, b)
            far_rows[s, j] = owner * CAP + (t - owner * b > low_s[0, owner]).astype(i32)
        return carry

    lax.fori_loop(0, b, far_index, 0)
    near_slots(b // 4, b)
    each_peer(lambda d: geo_cp(d).wait())

    def far_geo(t):
        g = geo_in[t].astype(f32)
        return [(g[q : q + 3] + g[q + 3 : q + 6], g[q + 6 : q + 9] + g[q + 9 : q + 12]) for q in (0, 12)]

    def far_table(t, carry):
        for i in range(2):
            for c, g in enumerate(far_geo(t * 2 + i)):
                far_feats[(t * 2 + i) * CAP + c] = source_features(*g).astype(bf16)
        return carry

    lax.fori_loop(0, n // 2, far_table, 0)

    def far_slot(s, carry):
        row_tiles(far_rows, s, near * v, wts[s], far_feats, tiles)
        return carry

    lax.fori_loop(0, b, far_slot, 0, unroll=2)

    def near_sum(source):
        def step(s, carry):
            acc[s] = contract(near_rows, s, 0, source, tiles)
            return carry

        lax.fori_loop(0, b, step, 0, unroll=2)

    near_sum(field)

    def finish(i, box, write):
        lo, hi = cuts[i]
        row = lax.broadcasted_iota(i32, (hi - lo, v), 0) + lo

        def step(s, e):
            total = acc[s, lo:hi] + contract(far_rows, s, near * v, box[i], tiles)
            shade = jnp.broadcast_to(geo[s, 12:13, :], (hi - lo, v))
            for c in range(COLORS - 2, -1, -1):
                shade = jnp.where(row < (c + 1) * (ch // COLORS), geo[s, 10 + c : 11 + c, :], shade)
            val = total * shade
            keep = val if hi <= ch else jnp.where(row < ch, val, 0.0)
            write(s, lo, hi, val.astype(bf16))
            return e + jnp.sum(keep * keep, axis=0, keepdims=True) * geo[s, 9:10, :]

        return lambda e: lax.fori_loop(0, b, step, e, unroll=2)

    def planes(source, out, i):
        lo, hi = cuts[i]
        top = min(hi, ch)
        out[lo:top] = jnp.swapaxes(source[:, lo:hi], 0, 1)[0 : top - lo]

    def keep(ref):
        def write(s, lo, hi, val):
            ref[s, lo:hi] = val

        return write

    e1 = jnp.zeros((1, v), f32)
    for i in range(k):
        each_peer(lambda d: first_cp[i](d).wait())
        e1 = finish(i, box_in, keep(one))(e1)
        pack(put_field(i, one))
        each_peer(lambda d: second_cp[i](d).start())
        planes(one, out1, i)
    one_cp = pltpu.make_async_copy(out1, one_hbm, loc.at[0])
    one_cp.start()
    near_sum(one)
    e2 = jnp.zeros((1, v), f32)
    for i in range(k):
        each_peer(lambda d: second_cp[i](d).wait())
        e2 = finish(i, box_in2, keep(two))(e2)
        if i < k - 1:
            planes(two, out2, i)
    en[...] = jnp.concatenate([e1, e2], axis=0)
    en_in[me] = en[...]
    each_peer(lambda d: en_cp(d).start())
    planes(two, out2, k - 1)
    two_cp = pltpu.make_async_copy(out2, two_hbm, loc.at[1])
    two_cp.start()
    one_cp.wait()
    each_peer(lambda d: en_cp(d).wait())
    total = jnp.sum(en_in[...], axis=0) * (1.0 / (n * b * v * ch))
    energy_ref[0] = jnp.sum(total[0:1])
    energy_ref[1] = jnp.sum(total[1:2])
    two_cp.wait()


def body(transfer, positions, normals, area, albedo, pairs, home):
    n = lax.axis_size(AXES)
    b, ch, v = transfer.shape
    far = pairs.shape[1] - NEAR
    rows = -(-ch // 16) * 16
    cut = -(-rows // 32) * 16
    cuts = ((0, cut), (cut, rows))
    bf16, f32, i32 = jnp.bfloat16, jnp.float32, jnp.int32
    lanes = -(-n // 128) * 128

    smem = pl.BlockSpec(memory_space=pltpu.SMEM)
    hbm = pl.BlockSpec(memory_space=pl.ANY)
    sem = pltpu.SemaphoreType.DMA((n,))
    boxes = [pltpu.VMEM((n * CAP, hi - lo, v), bf16) for lo, hi in cuts]
    one, two, energies = pl.pallas_call(
        functools.partial(bounce_kernel, n, lax.axis_size("gy"), ch, cuts),
        name="bounces",
        in_specs=[smem, smem] + [hbm] * 5,
        out_specs=[hbm, hbm, smem],
        out_shape=[
            jax.ShapeDtypeStruct((ch, b, v), bf16),
            jax.ShapeDtypeStruct((ch, b, v), bf16),
            jax.ShapeDtypeStruct((2,), f32),
        ],
        scratch_shapes=[
            pltpu.SMEM((b, NEAR), i32),
            pltpu.SMEM((b, far), i32),
            pltpu.SMEM((b, far), i32),
            pltpu.SMEM((1, lanes), i32),
            pltpu.SMEM((n, 1, lanes), i32),
            pltpu.VMEM((ch, b, v), bf16),
            pltpu.VMEM((3, b, v), f32),
            pltpu.VMEM((3, b, v), f32),
            pltpu.VMEM((b, v), f32),
            pltpu.VMEM((3, b, v), f32),
            pltpu.VMEM((b, 16, v), f32),
            pltpu.VMEM((b, 16, v), bf16),
            pltpu.VMEM((b, rows, v), bf16),
            pltpu.VMEM((n, 24, v), bf16),
            pltpu.VMEM((n, 24, v), bf16),
            pltpu.VMEM((b, v, v), bf16),
            pltpu.VMEM((n * CAP, v, v), bf16),
            pltpu.VMEM((b, v, 6 * v), bf16),
            pltpu.VMEM((b, (NEAR + far) * v, v), bf16),
            pltpu.VMEM((2, 1, lanes), i32),
            pltpu.VMEM((n, 1, lanes), i32),
            pltpu.VMEM((b, rows, v), f32),
            pltpu.VMEM((b, rows, v), bf16),
            pltpu.VMEM((b, rows, v), bf16),
            pltpu.VMEM((ch, b, v), bf16),
            pltpu.VMEM((ch, b, v), bf16),
            pltpu.VMEM((2, v), f32),
            pltpu.VMEM((n, 2, v), f32),
        ]
        + boxes * 3
        + [pltpu.SemaphoreType.DMA((6,))]
        + [sem] * (6 + 4 * len(cuts)),
        compiler_params=pltpu.CompilerParams(
            collective_id=0, has_side_effects=True, vmem_limit_bytes=VMEM_LIMIT
        ),
    )(
        pairs, home,
        jnp.swapaxes(transfer, 0, 1), jnp.swapaxes(positions, 0, 1),
        jnp.swapaxes(normals, 0, 1), area, jnp.swapaxes(albedo, 0, 1),
    )
    return jnp.swapaxes(one, 0, 1), jnp.swapaxes(two, 0, 1), energies


def solution(mesh):
    return jax.shard_map(
        body,
        mesh=mesh,
        in_specs=(
            P(AXES, None, None),
            P(AXES, None, None),
            P(AXES, None, None),
            P(AXES, None),
            P(AXES, None, None),
            P(AXES, None),
            P(),
        ),
        out_specs=(P(AXES, None, None), P(AXES, None, None), P()),
        check_vma=False,
    )
```

time: 112 us -> 92.2 us (0.82)
  starting transfers between devices: 7.33 us -> 0 us
  local copies, waits for them, and re-layouts: 8.6 us -> 2.99 us
  other arithmetic: 4.54 us -> 0 us
  Pallas kernels: 89.8 us -> 88.4 us
  waiting for transfers between devices: 1.24 us -> 0 us
    all_to_all x1 -> x0, starting transfers between devices: 7.33 us -> none  [body(): lax.all_to_all(jnp.stack([low, high], axis=1), AXES, split_axis=0, concat...]
    unnamed x14 -> x7, local copies, waits for them, and re-layouts: 6.78 us -> 2.99 us
    reduce_sum x3 -> x0, other arithmetic: 1.78 us -> none  [the longest x1 1.24 us: body(): slot_ids = jnp.sum(jnp.where(pairs[:, :, None] == ids, home, 0), axis=2)]
    pallas_call x1, Pallas kernels: 89.8 us -> 88.4 us  [body(): pl.pallas_call(functools.partial(bounce_kernel, n, lax.axis_size('gy'), c...]
    all_to_all x1 -> x0, waiting for transfers between devices: 1.24 us -> none  [body(): lax.all_to_all(jnp.stack([low, high], axis=1), AXES, split_axis=0, concat...]
    all_to_all x2 -> x0, local copies, waits for them, and re-layouts: 1.2 us -> none  [body(): lax.all_to_all(jnp.stack([low, high], axis=1), AXES, split_axis=0, concat...]
  transfers between devices with their start and end apart: 1 -> 0, of which waited for: 1 -> 0; matrix products, arithmetic and copies ran while one was open for 5% -> 0% of each run, Pallas kernels for 0% -> 0%
where the time goes in v1:
time: 92.2 us; the launch traced here: 92 us
  Pallas kernels  88.4 us (96%)
  local copies, waits for them, and re-layouts  2.99 us (3%)
    pallas_call x1, Pallas kernels, body(): pl.pallas_call(functools.partial(bounce_kernel, n, lax.axis_size('gy'), c...  88.4 us
    unnamed x7, local copies, waits for them, and re-layouts  2.99 us

profile of v1, /device:TPU:0, one launch (start us, length us, event | category | flops | bytes accessed | tf_op | source)
XLA Modules:
  0.0 92.0 jit_solution(14708800787766193222)
XLA Ops:
  0.6 88.4 %bounces.1 = (bf16[75,16,128]{2,1,0:T(8,128)(2,1)}, bf16[75,16,128]{2,1,0:T(8,128)(2,1)}, f32[2]{0:T(128)}) custom-call(s32[16,40]{1,0:T(8,128)} %pairs.1, s32[512]{0:T(512)} %home.1, bf16[75,16,128]{2,1,0:T(8,128)(2,1)} %bitcast.6, f32[3,16,128]{2,1,0:T(8,128)} %bitcast.9, f32[3,16,128]{2,1,0:T(8,128)} %bitcast.10, f32[16,128]{1,0:T(8,128)} %area.1, ...), custom_call_target="tpu_custom_call" | custom-call | tf_op jit(solution)/shard_map/bounces/pallas_call | solution.py:394
  89.0 0.0 copy-start
  89.0 1.7 %copy.13 = bf16[16,75,128]{2,0,1:T(8,128)(2,1)} copy(bf16[16,75,128]{2,0,1:T(8,128)(2,1)} %bitcast.8) | data formatting | bytes 614400
  90.8 0.0 copy-done
  90.8 0.0 copy-start.1
  90.8 0.7 copy.14
  91.5 0.0 copy-done.1
  91.5 0.5 copy.15
Async XLA Ops:
  89.0 1.8 %copy-start = (bf16[75,16,128]{2,1,0:T(8,128)(2,1)S(1)}, bf16[75,16,128]{2,1,0:T(8,128)(2,1)}, u32[]{:S(2)}) copy-start(bf16[75,16,128]{2,1,0:T(8,128)(2,1)} %get-tuple-element.7) | copy-start | bytes 921604
  90.8 0.7 copy-start.1

commit v2 on v1

v2 whole, which is shorter than its diff:
```python
import functools

import jax
import jax.numpy as jnp
from jax import lax
from jax.experimental import pallas as pl
from jax.experimental.pallas import tpu as pltpu
from jax.sharding import PartitionSpec as P

COLORS = 3
NEAR = 16
CAP = 2
AXES = ("gx", "gy")
VMEM_LIMIT = 62 * 1024 * 1024
MESH = pl.DeviceIdType.MESH


def split3(f):
    hi = f.astype(jnp.bfloat16).astype(jnp.float32)
    rest = f - hi
    mid = rest.astype(jnp.bfloat16).astype(jnp.float32)
    return hi, mid, rest - mid


def source_features(pos, m):
    lanes = pos.shape[1]
    sq = jnp.sum(pos * pos, axis=0, keepdims=True)
    d = -jnp.sum(m * pos, axis=0, keepdims=True)
    hi, mid, lo = split3(jnp.concatenate([pos, sq, m, d], axis=0))
    ones = jnp.ones((8, lanes), jnp.float32)
    half = jnp.concatenate([hi, hi, hi, mid, mid, lo, ones, jnp.zeros_like(ones)], axis=0)
    return jnp.concatenate([half, half], axis=0).T


def receiver_weights(pos, nrm):
    lanes = pos.shape[1]
    zero3 = jnp.zeros((3, lanes), jnp.float32)
    zero1 = jnp.zeros((1, lanes), jnp.float32)
    one1 = jnp.ones((1, lanes), jnp.float32)
    zero5 = jnp.zeros((5, lanes), jnp.float32)
    zero8 = jnp.zeros((8, lanes), jnp.float32)

    def column(feat, const):
        hi, mid, lo = split3(feat)
        chi, cmid, clo = split3(const)
        return jnp.concatenate(
            [hi, mid, lo, hi, mid, hi, jnp.concatenate([chi, cmid, clo, zero5], axis=0), zero8],
            axis=0,
        )

    dist = column(
        jnp.concatenate([-2.0 * pos, one1, zero3, zero1], axis=0),
        jnp.sum(pos * pos, axis=0, keepdims=True) + 1.0,
    )
    along_p = column(
        jnp.concatenate([nrm, zero1, zero3, zero1], axis=0),
        -jnp.sum(nrm * pos, axis=0, keepdims=True),
    )
    along_q = column(jnp.concatenate([zero3, zero1, pos, one1], axis=0), zero1)
    return jnp.concatenate([dist, along_p, along_q], axis=1)


def block_diag(w):
    z = jnp.zeros_like(w)
    return jnp.concatenate(
        [jnp.concatenate([w, z], axis=1), jnp.concatenate([z, w], axis=1)], axis=0
    ).astype(jnp.bfloat16)


def row_tiles(rows_ref, slot, base, weights, feats, tiles, side):
    v = tiles.shape[-1] // 2
    first = lax.broadcasted_iota(jnp.int32, (v, v), 1) < v // 2
    for i in range(rows_ref.shape[1] // 4):
        t = [rows_ref[slot, i * 4 + j] for j in range(4)]
        x = jnp.concatenate(
            [
                jnp.where(first, feats[t[0]], feats[t[1]]),
                jnp.where(first, feats[t[2]], feats[t[3]]),
            ],
            axis=0,
        )
        g = jnp.dot(x, weights, preferred_element_type=jnp.float32)
        for j in range(4):
            r, c = (j // 2) * v, (j % 2) * 3 * v
            dist = g[r : r + v, c : c + v]
            ap = g[r : r + v, c + v : c + 2 * v]
            aq = g[r : r + v, c + 2 * v : c + 3 * v]
            f = jnp.maximum(ap, 0.0) * jnp.maximum(aq, 0.0) / (dist * dist)
            at = base + (i * 4 + j) * v
            tiles[at : at + v, side * v : (side + 1) * v] = f.astype(jnp.bfloat16)


def contract(rows_ref, i, base, field, tiles):
    v = tiles.shape[-1] // 2
    count = rows_ref.shape[1]
    picked = jnp.concatenate(
        [
            jnp.concatenate([field[rows_ref[2 * i + side, j]] for j in range(count)], axis=1)
            for side in range(2)
        ],
        axis=0,
    )
    both = jnp.dot(
        picked, tiles[i, base : base + count * v, :], preferred_element_type=jnp.float32
    )
    rows = both.shape[0] // 2
    return both[0:rows, 0:v], both[rows:, v:]


def bounce_kernel(
    n, ny, ch, cuts,
    pairs, home, transfer, positions, normals, area, albedo,
    one_hbm, two_hbm, energy_ref,
    *scratch,
):
    (
        near_rows, far_ids, far_rows, low_s, req_s,
        tr, raw_pos, raw_nrm, raw_area, raw_alb, geo,
        wire_planes, guest_planes, wire, guest_wire, field,
        geo_own, geo_fwd, geo_in, near_feats, far_feats, wts, tiles,
        req_v, req_in, acc, one, two, out1, out2, en, en_in,
    ) = scratch[:32]
    k = len(cuts)
    groups = [scratch[32 + i * k : 32 + (i + 1) * k] for i in range(7)]
    box_own, box_fwd, box_in, box_in2, guest, planes_in, planes_in2 = groups
    loc, stat_s, stat_r, req_sems, en_sems = scratch[32 + 7 * k : 37 + 7 * k]
    peer_sems = scratch[37 + 7 * k :]
    bf16, f32, i32 = jnp.bfloat16, jnp.float32, jnp.int32

    gx, gy = lax.axis_index("gx"), lax.axis_index("gy")
    me = gx * ny + gy
    h, nh = ny // 2, n // 2
    side = lax.div(gy, h)
    mate_y = lax.rem(gy + h, ny)
    mate = gx * ny + mate_y
    spot = gx * h + gy - side * h
    b, v = area.shape
    near = near_rows.shape[1]
    far = far_ids.shape[1]

    def peer(d):
        t = lax.rem(me + d, n)
        return (lax.div(t, ny), lax.rem(t, ny))

    def side_peer(d):
        t = lax.rem(spot + d, nh)
        return t, (lax.div(t, h), side * h + lax.rem(t, h))

    def each(count, fn):
        def step(d, carry):
            fn(d)
            return carry

        lax.fori_loop(1, count, step, 0)

    def pair(ref, t):
        return ref.at[pl.ds(t * CAP, CAP)]

    class Spread:
        def __init__(self, sems, src, dst):
            self.sems, self.src, self.dst = sems, src, dst

        def copy(self, d):
            t, dev = side_peer(d)
            return pltpu.make_async_remote_copy(
                src_ref=self.src(t), dst_ref=self.dst,
                send_sem=self.sems.at[0, d], recv_sem=self.sems.at[1, d],
                device_id=dev, device_id_type=MESH,
            )

        def start(self):
            each(nh, lambda d: self.copy(d).start())

        def wait(self):
            each(nh, lambda d: self.copy(d).wait())

    def to_mate(i, src, dst):
        return pltpu.make_async_remote_copy(
            src_ref=src, dst_ref=dst, send_sem=stat_s.at[i], recv_sem=stat_r.at[i],
            device_id=(gx, mate_y), device_id_type=MESH,
        )

    def en_copy(d):
        return pltpu.make_async_remote_copy(
            src_ref=en, dst_ref=en_in.at[me],
            send_sem=en_sems.at[0, d], recv_sem=en_sems.at[1, d],
            device_id=peer(d), device_id_type=MESH,
        )

    req_x = Spread(req_sems, lambda t: req_v.at[0], req_in.at[spot])
    geo_x = [
        Spread(peer_sems[0], lambda t: geo_own.at[t], geo_in.at[me]),
        Spread(peer_sems[1], lambda t: geo_fwd.at[t], geo_in.at[mate]),
    ]

    def field_x(i, base, box):
        return [
            Spread(peer_sems[base], lambda t: pair(box_own[i], t), pair(box[i], me)),
            Spread(peer_sems[base + 1], lambda t: pair(box_fwd[i], t), pair(box[i], mate)),
        ]

    first_x = [field_x(i, 2 + 2 * i, box_in) for i in range(k)]
    second_x = [field_x(i, 2 + 2 * k + 2 * i, box_in2) for i in range(k)]
    tops = [min(hi, ch) for lo, hi in cuts]
    geo_m = to_mate(0, wire_planes, guest_planes)
    first_m = [
        to_mate(1 + i, tr.at[pl.ds(lo, tops[i] - lo)], planes_in[i])
        for i, (lo, hi) in enumerate(cuts)
    ]
    second_m = [
        to_mate(1 + k + i, out1.at[pl.ds(lo, tops[i] - lo)], planes_in2[i])
        for i, (lo, hi) in enumerate(cuts)
    ]

    barrier = pltpu.get_barrier_semaphore()
    each(n, lambda d: pl.semaphore_signal(barrier, inc=1, device_id=peer(d), device_id_type=MESH))
    loads = [
        pltpu.make_async_copy(src, dst, loc.at[i])
        for i, (src, dst) in enumerate(
            [
                (positions, raw_pos), (normals, raw_nrm), (area, raw_area),
                (albedo, raw_alb), (transfer, tr),
            ]
        )
    ]
    for cp in loads:
        cp.start()

    lanes = req_v.shape[2]
    floor = lax.broadcasted_iota(i32, (1, lanes), 1) * b

    def scan(s, carry):
        low, high = carry
        for j in range(near):
            near_rows[s, j] = lax.rem(home[pairs[s, j]], b)
        for j in range(far):
            t = home[pairs[s, near + j]]
            far_ids[s, j] = t
            x = t - floor
            ok = (x >= 0) & (x < b)
            low = jnp.minimum(low, jnp.where(ok, x, b - 1))
            high = jnp.maximum(high, jnp.where(ok, x, 0))
        return low, high

    low, high = lax.fori_loop(
        0, b, scan, (jnp.full((1, lanes), b - 1, i32), jnp.zeros((1, lanes), i32))
    )
    req_v[0] = low + high * b
    req_v[1] = low
    req_in[spot] = low + high * b
    low_cp = pltpu.make_async_copy(req_v.at[1], low_s, loc.at[5])
    low_cp.start()

    for cp in loads[:4]:
        cp.wait()
    m = raw_nrm[...] * (raw_area[...] * (1.0 / jnp.pi))[None]
    p_hi, p_mid, _ = split3(raw_pos[...])
    m_hi, m_mid, _ = split3(m)
    geo[...] = jnp.swapaxes(
        jnp.concatenate(
            [raw_pos[...], m, raw_nrm[...], raw_area[...][None], raw_alb[...],
             jnp.zeros((3, b, v), f32)], axis=0
        ),
        0, 1,
    )
    planes = jnp.concatenate([p_hi, p_mid, m_hi, m_mid], axis=0)
    wire_planes[...] = planes.astype(bf16)
    wire[...] = jnp.swapaxes(
        jnp.concatenate([planes, jnp.zeros((4, b, v), f32)], axis=0), 0, 1
    ).astype(bf16)
    loads[4].wait()

    def rows_of(source, i, base):
        lo, hi = cuts[i]
        part = source[lo - base : tops[i] - base]
        if hi > ch:
            part = jnp.concatenate([part, jnp.zeros((hi - ch, b, v), bf16)], axis=0)
        return jnp.swapaxes(part, 0, 1)

    for i, (lo, hi) in enumerate(cuts):
        field[:, lo:hi] = rows_of(tr, i, 0)

    def table(read, count, feats):
        def step(t, carry):
            for i in range(4):
                feats[t * 4 + i] = source_features(*read(t * 4 + i)).astype(bf16)
            return carry

        lax.fori_loop(0, count // 4, step, 0)

    table(lambda t: (geo[t, 0:3], geo[t, 3:6]), b, near_feats)

    def near_slots(lo, hi):
        def step(i, carry):
            for side in range(2):
                s = 2 * i + side
                w = block_diag(receiver_weights(geo[s, 0:3], geo[s, 6:9]))
                wts[s] = w
                row_tiles(near_rows, s, 0, w, near_feats, tiles.at[i], side)
            return carry

        lax.fori_loop(lo // 2, hi // 2, step, 0)

    pl.semaphore_wait(barrier, n - 1)
    req_x.start()
    for cp in [geo_m] + first_m[:1]:
        cp.start()
    near_slots(0, b // 4)
    for box in (geo_in,) + tuple(box_in) + tuple(box_in2):
        width = box.shape[0] // n
        for c in range(width):
            box[me * width + c] = jnp.zeros(box.shape[1:], box.dtype)
    req_x.wait()
    ask_cp = pltpu.make_async_copy(req_in, req_s, loc.at[0])
    ask_cp.start()
    ask_cp.wait()

    def asked(t, dev):
        r = req_s[t, 0, dev]
        hi = lax.div(r, b)
        return r - hi * b, hi

    def pack(dev, put):
        def step(t, carry):
            put(t, *asked(t, dev))
            return carry

        lax.fori_loop(0, nh, step, 0)

    def geo_pair(source, x, y):
        return jnp.concatenate([source[x, 0:12], source[y, 0:12]], axis=0)

    def send_geo(x, dev, source, out):
        def put(t, p, q):
            out[t] = geo_pair(source, p, q)

        pack(dev, put)
        x.start()

    def send_field(x, dev, read, out):
        def put(t, p, q):
            out[t * CAP] = read(p)
            out[t * CAP + 1] = read(q)

        pack(dev, put)
        x.start()

    def send_own(i, x, source):
        lo, hi = cuts[i]
        send_field(x[0], me, lambda t: source[t, lo:hi], box_own[i])

    def send_guest(i, x, m, source, box):
        m.wait()
        guest[i][...] = rows_of(source[i], i, cuts[i][0])
        send_field(x[1], mate, lambda t: guest[i][t], box_fwd[i])
        for c, t in enumerate(asked(spot, mate)):
            box[i][mate * CAP + c] = guest[i][t]

    send_geo(geo_x[0], me, wire, geo_own)
    geo_m.wait()
    guest_wire[...] = jnp.swapaxes(
        jnp.concatenate([guest_planes[...].astype(f32), jnp.zeros((4, b, v), f32)], axis=0), 0, 1
    ).astype(bf16)
    send_geo(geo_x[1], mate, guest_wire, geo_fwd)
    for cp in first_m[1:]:
        cp.start()
    geo_in[mate] = geo_pair(guest_wire, *asked(spot, mate))
    send_own(0, first_x[0], field)

    low_cp.wait()

    def far_index(s, carry):
        for j in range(far):
            t = far_ids[s, j]
            owner = lax.div(t, b)
            far_rows[s, j] = owner * CAP + (t - owner * b > low_s[0, owner]).astype(i32)
        return carry

    lax.fori_loop(0, b, far_index, 0)
    near_slots(b // 4, 3 * b // 4)
    near_slots(3 * b // 4, b)
    def near_sum(source):
        def step(i, carry):
            acc[2 * i], acc[2 * i + 1] = contract(near_rows, i, 0, source, tiles)
            return carry

        lax.fori_loop(0, b // 2, step, 0, unroll=4)

    near_sum(field)
    for x in geo_x:
        x.wait()
    send_guest(0, first_x[0], first_m[0], planes_in, box_in)
    for i in range(1, k):
        send_own(i, first_x[i], field)

    def far_geo(t):
        g = geo_in[t].astype(f32)
        return [(g[q : q + 3] + g[q + 3 : q + 6], g[q + 6 : q + 9] + g[q + 9 : q + 12]) for q in (0, 12)]

    def far_table(t, carry):
        for i in range(4):
            for c, g in enumerate(far_geo(t * 4 + i)):
                far_feats[(t * 4 + i) * CAP + c] = source_features(*g).astype(bf16)
        return carry

    lax.fori_loop(0, n // 4, far_table, 0)

    def far_slot(i, carry):
        for side in range(2):
            s = 2 * i + side
            row_tiles(far_rows, s, near * v, wts[s], far_feats, tiles.at[i], side)
        return carry

    lax.fori_loop(0, b // 8, far_slot, 0)
    for i in range(1, k):
        send_guest(i, first_x[i], first_m[i], planes_in, box_in)
    lax.fori_loop(b // 8, b // 2, far_slot, 0)

    def finish(i, box, write):
        lo, hi = cuts[i]
        row = lax.broadcasted_iota(i32, (hi - lo, v), 0) + lo

        def step(pair_id, e):
            sums = contract(far_rows, pair_id, near * v, box[i], tiles)
            for side in range(2):
                s = 2 * pair_id + side
                total = acc[s, lo:hi] + sums[side]
                shade = jnp.broadcast_to(geo[s, 12:13, :], (hi - lo, v))
                for c in range(COLORS - 2, -1, -1):
                    shade = jnp.where(
                        row < (c + 1) * (ch // COLORS), geo[s, 10 + c : 11 + c, :], shade
                    )
                val = total * shade
                keep = val if hi <= ch else jnp.where(row < ch, val, 0.0)
                write(s, lo, hi, val.astype(bf16))
                e = e + jnp.sum(keep * keep, axis=0, keepdims=True) * geo[s, 9:10, :]
            return e

        return lambda e: lax.fori_loop(0, b // 2, step, e, unroll=4)

    def to_planes(source, out, i):
        lo, hi = cuts[i]
        out[lo : tops[i]] = jnp.swapaxes(source[:, lo:hi], 0, 1)[0 : tops[i] - lo]

    def keep(ref):
        def write(s, lo, hi, val):
            ref[s, lo:hi] = val

        return write

    e1 = jnp.zeros((1, v), f32)
    for i in range(k):
        for x in first_x[i]:
            x.wait()
        e1 = finish(i, box_in, keep(one))(e1)
        to_planes(one, out1, i)
        second_m[i].start()
        send_own(i, second_x[i], one)
    one_cp = pltpu.make_async_copy(out1, one_hbm, loc.at[0])
    one_cp.start()
    send_guest(0, second_x[0], second_m[0], planes_in2, box_in2)
    near_sum(one)
    for i in range(1, k):
        send_guest(i, second_x[i], second_m[i], planes_in2, box_in2)
    e2 = jnp.zeros((1, v), f32)
    for i in range(k):
        for x in second_x[i]:
            x.wait()
        e2 = finish(i, box_in2, keep(two))(e2)
        if i < k - 1:
            to_planes(two, out2, i)
    en[...] = jnp.concatenate([e1, e2], axis=0)
    en_in[me] = en[...]
    each(n, lambda d: en_copy(d).start())
    to_planes(two, out2, k - 1)
    two_cp = pltpu.make_async_copy(out2, two_hbm, loc.at[1])
    two_cp.start()
    one_cp.wait()
    each(n, lambda d: en_copy(d).wait())
    total = jnp.sum(en_in[...], axis=0) * (1.0 / (n * b * v * ch))
    energy_ref[0] = jnp.sum(total[0:1])
    energy_ref[1] = jnp.sum(total[1:2])
    two_cp.wait()


def body(transfer, positions, normals, area, albedo, pairs, home):
    n = lax.axis_size(AXES)
    b, ch, v = transfer.shape
    far = pairs.shape[1] - NEAR
    rows = -(-ch // 16) * 16
    cut = -(-rows // 32) * 16
    cuts = ((0, cut), (cut, rows))
    bf16, f32, i32 = jnp.bfloat16, jnp.float32, jnp.int32
    lanes = -(-n // 128) * 128

    smem = pl.BlockSpec(memory_space=pltpu.SMEM)
    hbm = pl.BlockSpec(memory_space=pl.ANY)
    nh = n // 2
    sem = pltpu.SemaphoreType.DMA((2, nh))
    sizes = [hi - lo for lo, hi in cuts]
    boxes = [pltpu.VMEM((nh * CAP, size, v), bf16) for size in sizes] * 2
    boxes += [pltpu.VMEM((n * CAP, size, v), bf16) for size in sizes] * 2
    boxes += [pltpu.VMEM((b, size, v), bf16) for size in sizes]
    boxes += [pltpu.VMEM((min(hi, ch) - lo, b, v), bf16) for lo, hi in cuts] * 2
    one, two, energies = pl.pallas_call(
        functools.partial(bounce_kernel, n, lax.axis_size("gy"), ch, cuts),
        name="bounces",
        in_specs=[smem, smem] + [hbm] * 5,
        out_specs=[hbm, hbm, smem],
        out_shape=[
            jax.ShapeDtypeStruct((ch, b, v), bf16),
            jax.ShapeDtypeStruct((ch, b, v), bf16),
            jax.ShapeDtypeStruct((2,), f32),
        ],
        scratch_shapes=[
            pltpu.SMEM((b, NEAR), i32),
            pltpu.SMEM((b, far), i32),
            pltpu.SMEM((b, far), i32),
            pltpu.SMEM((1, lanes), i32),
            pltpu.SMEM((nh, 1, lanes), i32),
            pltpu.VMEM((ch, b, v), bf16),
            pltpu.VMEM((3, b, v), f32),
            pltpu.VMEM((3, b, v), f32),
            pltpu.VMEM((b, v), f32),
            pltpu.VMEM((3, b, v), f32),
            pltpu.VMEM((b, 16, v), f32),
            pltpu.VMEM((12, b, v), bf16),
            pltpu.VMEM((12, b, v), bf16),
            pltpu.VMEM((b, 16, v), bf16),
            pltpu.VMEM((b, 16, v), bf16),
            pltpu.VMEM((b, rows, v), bf16),
            pltpu.VMEM((nh, 24, v), bf16),
            pltpu.VMEM((nh, 24, v), bf16),
            pltpu.VMEM((n, 24, v), bf16),
            pltpu.VMEM((b, v, v), bf16),
            pltpu.VMEM((n * CAP, v, v), bf16),
            pltpu.VMEM((b, v, 6 * v), bf16),
            pltpu.VMEM((b // 2, (NEAR + far) * v, 2 * v), bf16),
            pltpu.VMEM((2, 1, lanes), i32),
            pltpu.VMEM((nh, 1, lanes), i32),
            pltpu.VMEM((b, rows, v), f32),
            pltpu.VMEM((b, rows, v), bf16),
            pltpu.VMEM((b, rows, v), bf16),
            pltpu.VMEM((ch, b, v), bf16),
            pltpu.VMEM((ch, b, v), bf16),
            pltpu.VMEM((2, v), f32),
            pltpu.VMEM((n, 2, v), f32),
        ]
        + boxes
        + [pltpu.SemaphoreType.DMA((6,))]
        + [pltpu.SemaphoreType.DMA((1 + 2 * len(cuts),))] * 2
        + [sem, pltpu.SemaphoreType.DMA((2, n))]
        + [sem] * (2 + 4 * len(cuts)),
        compiler_params=pltpu.CompilerParams(
            collective_id=0, has_side_effects=True, vmem_limit_bytes=VMEM_LIMIT
        ),
    )(
        pairs, home,
        jnp.swapaxes(transfer, 0, 1), jnp.swapaxes(positions, 0, 1),
        jnp.swapaxes(normals, 0, 1), area, jnp.swapaxes(albedo, 0, 1),
    )
    return jnp.swapaxes(one, 0, 1), jnp.swapaxes(two, 0, 1), energies


def solution(mesh):
    return jax.shard_map(
        body,
        mesh=mesh,
        in_specs=(
            P(AXES, None, None),
            P(AXES, None, None),
            P(AXES, None, None),
            P(AXES, None),
            P(AXES, None, None),
            P(AXES, None),
            P(),
        ),
        out_specs=(P(AXES, None, None), P(AXES, None, None), P()),
        check_vma=False,
    )
```

time: 92.2 us -> 81.4 us (0.88)
  Pallas kernels: 88.4 us -> 77.6 us
    pallas_call x1, Pallas kernels: 88.4 us -> 77.6 us  [body(): pl.pallas_call(functools.partial(bounce_kernel, n, lax.axis_size('gy'), c...]
where the time goes in v2:
time: 81.4 us; the launch traced here: 81.2 us
  Pallas kernels  77.6 us (95%)
  local copies, waits for them, and re-layouts  2.99 us (4%)
    pallas_call x1, Pallas kernels, body(): pl.pallas_call(functools.partial(bounce_kernel, n, lax.axis_size('gy'), c...  77.6 us
    unnamed x7, local copies, waits for them, and re-layouts  2.99 us

profile of v2, /device:TPU:0, one launch (start us, length us, event | category | flops | bytes accessed | tf_op | source)
XLA Modules:
  0.0 81.2 jit_solution(880814538375784485)
XLA Ops:
  0.6 77.6 %bounces.1 = (bf16[75,16,128]{2,1,0:T(8,128)(2,1)}, bf16[75,16,128]{2,1,0:T(8,128)(2,1)}, f32[2]{0:T(128)}) custom-call(s32[16,40]{1,0:T(8,128)} %pairs.1, s32[512]{0:T(512)} %home.1, bf16[75,16,128]{2,1,0:T(8,128)(2,1)} %bitcast.6, f32[3,16,128]{2,1,0:T(8,128)} %bitcast.9, f32[3,16,128]{2,1,0:T(8,128)} %bitcast.10, f32[16,128]{1,0:T(8,128)} %area.1, ...), custom_call_target="tpu_custom_call" | custom-call | tf_op jit(solution)/shard_map/bounces/pallas_call | solution.py:505
  78.2 0.0 copy-start
  78.2 1.7 %copy.13 = bf16[16,75,128]{2,0,1:T(8,128)(2,1)} copy(bf16[16,75,128]{2,0,1:T(8,128)(2,1)} %bitcast.8) | data formatting | bytes 614400
  80.0 0.0 copy-done
  80.0 0.0 copy-start.1
  80.0 0.7 copy.14
  80.7 0.0 copy-done.1
  80.7 0.5 copy.15
Async XLA Ops:
  78.2 1.8 %copy-start = (bf16[75,16,128]{2,1,0:T(8,128)(2,1)S(1)}, bf16[75,16,128]{2,1,0:T(8,128)(2,1)}, u32[]{:S(2)}) copy-start(bf16[75,16,128]{2,1,0:T(8,128)(2,1)} %get-tuple-element.7) | copy-start | bytes 921604
  80.0 0.7 copy-start.1

commit v3 on v2

--- a/solution.py
+++ b/solution.py
@@ -151,7 +151,7 @@
             fn(d)
             return carry
 
-        lax.fori_loop(1, count, step, 0)
+        lax.fori_loop(1, count, step, 0, unroll=5)
 
     def pair(ref, t):
         return ref.at[pl.ds(t * CAP, CAP)]
@@ -325,7 +325,7 @@
             put(t, *asked(t, dev))
             return carry
 
-        lax.fori_loop(0, nh, step, 0)
+        lax.fori_loop(0, nh, step, 0, unroll=4)
 
     def geo_pair(source, x, y):
         return jnp.concatenate([source[x, 0:12], source[y, 0:12]], axis=0)
@@ -488,7 +488,7 @@
     b, ch, v = transfer.shape
     far = pairs.shape[1] - NEAR
     rows = -(-ch // 16) * 16
-    cut = -(-rows // 32) * 16
+    cut = 16
     cuts = ((0, cut), (cut, rows))
     bf16, f32, i32 = jnp.bfloat16, jnp.float32, jnp.int32
     lanes = -(-n // 128) * 128

time: 81.4 us -> 77.2 us (0.948)
  Pallas kernels: 77.6 us -> 73.4 us
    pallas_call x1, Pallas kernels: 77.6 us -> 73.4 us  [body(): pl.pallas_call(functools.partial(bounce_kernel, n, lax.axis_size('gy'), c...]
where the time goes in v3:
time: 77.2 us; the launch traced here: 77 us
  Pallas kernels  73.4 us (95%)
  local copies, waits for them, and re-layouts  2.99 us (4%)
    pallas_call x1, Pallas kernels, body(): pl.pallas_call(functools.partial(bounce_kernel, n, lax.axis_size('gy'), c...  73.4 us
    unnamed x7, local copies, waits for them, and re-layouts  2.99 us

profile of v3, /device:TPU:0, one launch (start us, length us, event | category | flops | bytes accessed | tf_op | source)
XLA Modules:
  0.0 77.0 jit_solution(16789833483664030080)
XLA Ops:
  0.6 73.4 %bounces.1 = (bf16[75,16,128]{2,1,0:T(8,128)(2,1)}, bf16[75,16,128]{2,1,0:T(8,128)(2,1)}, f32[2]{0:T(128)}) custom-call(s32[16,40]{1,0:T(8,128)} %pairs.1, s32[512]{0:T(512)} %home.1, bf16[75,16,128]{2,1,0:T(8,128)(2,1)} %bitcast.6, f32[3,16,128]{2,1,0:T(8,128)} %bitcast.9, f32[3,16,128]{2,1,0:T(8,128)} %bitcast.10, f32[16,128]{1,0:T(8,128)} %area.1, ...), custom_call_target="tpu_custom_call" | custom-call | tf_op jit(solution)/shard_map/bounces/pallas_call | solution.py:505
  74.0 0.0 copy-start
  74.0 1.7 %copy.13 = bf16[16,75,128]{2,0,1:T(8,128)(2,1)} copy(bf16[16,75,128]{2,0,1:T(8,128)(2,1)} %bitcast.8) | data formatting | bytes 614400
  75.8 0.0 copy-done
  75.8 0.0 copy-start.1
  75.8 0.7 copy.14
  76.5 0.0 copy-done.1
  76.5 0.5 copy.15
Async XLA Ops:
  74.0 1.8 %copy-start = (bf16[75,16,128]{2,1,0:T(8,128)(2,1)S(1)}, bf16[75,16,128]{2,1,0:T(8,128)(2,1)}, u32[]{:S(2)}) copy-start(bf16[75,16,128]{2,1,0:T(8,128)(2,1)} %get-tuple-element.7) | copy-start | bytes 921604
  75.8 0.7 copy-start.1

commit v4 on v3

--- a/solution.py
+++ b/solution.py
@@ -398,12 +398,12 @@
         return [(g[q : q + 3] + g[q + 3 : q + 6], g[q + 6 : q + 9] + g[q + 9 : q + 12]) for q in (0, 12)]
 
     def far_table(t, carry):
-        for i in range(4):
-            for c, g in enumerate(far_geo(t * 4 + i)):
-                far_feats[(t * 4 + i) * CAP + c] = source_features(*g).astype(bf16)
+        for i in range(8):
+            for c, g in enumerate(far_geo(t * 8 + i)):
+                far_feats[(t * 8 + i) * CAP + c] = source_features(*g).astype(bf16)
         return carry
 
-    lax.fori_loop(0, n // 4, far_table, 0)
+    lax.fori_loop(0, n // 8, far_table, 0)
 
     def far_slot(i, carry):
         for side in range(2):

time: 77.2 us -> 76.8 us (level)
  no operation moved by 1% of the time
where the time goes in v4:
time: 76.8 us; the launch traced here: 76.6 us
  Pallas kernels  73 us (95%)
  local copies, waits for them, and re-layouts  2.99 us (4%)
    pallas_call x1, Pallas kernels, body(): pl.pallas_call(functools.partial(bounce_kernel, n, lax.axis_size('gy'), c...  73 us
    unnamed x7, local copies, waits for them, and re-layouts  2.99 us

profile of v4, /device:TPU:0, one launch (start us, length us, event | category | flops | bytes accessed | tf_op | source)
XLA Modules:
  0.0 76.6 jit_solution(2022197626778089357)
XLA Ops:
  0.6 73.0 %bounces.1 = (bf16[75,16,128]{2,1,0:T(8,128)(2,1)}, bf16[75,16,128]{2,1,0:T(8,128)(2,1)}, f32[2]{0:T(128)}) custom-call(s32[16,40]{1,0:T(8,128)} %pairs.1, s32[512]{0:T(512)} %home.1, bf16[75,16,128]{2,1,0:T(8,128)(2,1)} %bitcast.6, f32[3,16,128]{2,1,0:T(8,128)} %bitcast.9, f32[3,16,128]{2,1,0:T(8,128)} %bitcast.10, f32[16,128]{1,0:T(8,128)} %area.1, ...), custom_call_target="tpu_custom_call" | custom-call | tf_op jit(solution)/shard_map/bounces/pallas_call | solution.py:505
  73.6 0.0 copy-start
  73.6 1.7 %copy.13 = bf16[16,75,128]{2,0,1:T(8,128)(2,1)} copy(bf16[16,75,128]{2,0,1:T(8,128)(2,1)} %bitcast.8) | data formatting | bytes 614400
  75.4 0.0 copy-done
  75.4 0.0 copy-start.1
  75.4 0.7 copy.14
  76.1 0.0 copy-done.1
  76.1 0.5 copy.15
Async XLA Ops:
  73.6 1.8 %copy-start = (bf16[75,16,128]{2,1,0:T(8,128)(2,1)S(1)}, bf16[75,16,128]{2,1,0:T(8,128)(2,1)}, u32[]{:S(2)}) copy-start(bf16[75,16,128]{2,1,0:T(8,128)(2,1)} %get-tuple-element.7) | copy-start | bytes 921604
  75.4 0.7 copy-start.1
